TPU v7x, 32 devices: a whole 2x2x4 slice. The times are simulated.
32 devices in a mesh: dp: 8 (over z, y), mp: 4 (over x, core).
Axes of the slice: x: 2, y: 2, z: 4, core: 2. Of those that a mesh axis runs over, the one named last changes fastest.
Arguments:
- tokens: bfloat16 [2048, 4096], P('dp', 'mp'), may hold values from -6 to 6
- router_weight: bfloat16 [4096, 64], P('mp'), may hold values from -1 to 1
- valid_count: int32 [8], P('dp'), may hold values from 64 to 256, as said below
- expert_id: int32 [2048], P('dp'), may hold values from 0 to 63, as said below
- slot_id: int32 [2048], P('dp'), may hold values from 0 to 5
Outputs:
- gates: float32 [2048], P('dp')
- dispatched: bfloat16 [384, 8, 4096], P('dp', None, 'mp')
Inputs may be any that keep to these rules, and one draw needn't show every extreme that they name: Group g's live tokens are its first valid_count[g] positions; the last group is full. Within one group no two positions share an expert and a slot. Flat slots expert_id * 6 + slot_id are held 48 in a row by one owner; one group's positions take at most 32 slots of any owner, and in every group some owner has 32 of its slots taken by live tokens.
All inputs are finite; a program needn't handle non-finite values.
Results may differ from a plain program's by a relative error of at most 0.001.
Values may be sent and summed in bfloat16 or wider, within the bound.
A program may use at most 64 MiB of HBM per device.

v0:
```python
import jax
import jax.numpy as jnp
from jax import lax
from jax.sharding import PartitionSpec as P

E = 64
ITERS = 5
CAP = 6


def dispatch(tokens, live, expert_id, slot_id):
    total_slots = E * CAP
    target = expert_id * CAP + slot_id
    placed = jnp.where(live, target, total_slots)
    buffer = (
        jnp.zeros((total_slots, tokens.shape[1]), jnp.bfloat16).at[placed].set(tokens, mode="drop")
    )
    return lax.all_to_all(buffer[:, None, :], "dp", split_axis=0, concat_axis=1, tiled=True)


def balance(logits, live, expert_id, total, column_sum):
    experts = logits.shape[1]
    affinity = jnp.exp(logits)
    weight = live.astype(jnp.float32)
    col_scale = jnp.ones((experts,), jnp.float32)
    row_scale = jnp.ones((logits.shape[0],), jnp.float32)
    for sweep in range(ITERS):
        row_scale = experts / jnp.sum(affinity * col_scale[None, :], axis=1)
        column = column_sum(jnp.sum(affinity * (weight * row_scale)[:, None], axis=0))
        col_scale = total / column
    chosen = expert_id[:, None] == jnp.arange(experts, dtype=jnp.int32)[None, :]
    picked = jnp.sum(jnp.where(chosen, affinity * col_scale[None, :], 0.0), axis=1)
    return weight * row_scale * picked


def local(tokens, router_weight, valid_count, expert_id, slot_id):
    rows = tokens.shape[0]
    live = jnp.arange(rows, dtype=jnp.int32) < valid_count[0]
    dispatched = None
    total = lax.psum(valid_count.astype(jnp.float32)[0], "dp")
    partial_logits = jnp.dot(tokens, router_weight, preferred_element_type=jnp.float32)
    logits = lax.psum(partial_logits, "mp")

    def group_sum(partial_value):
        return lax.psum(partial_value, "dp")

    gates = balance(logits, live, expert_id, total, group_sum)
    dispatched = dispatch(tokens, live, expert_id, slot_id)
    return (gates, dispatched)


def solution(mesh):
    placed = (P("dp", "mp"), P("mp", None), P("dp"), P("dp"), P("dp"))
    return jax.shard_map(
        local, mesh=mesh, in_specs=placed, out_specs=(P("dp"), P("dp", None, "mp")), check_vma=False
    )
```

profile of v0, /device:TPU:0, one launch (start us, length us, event | category | flops | bytes accessed | tf_op | source)
XLA Modules:
  0.0 163.1 jit_solution(8325949597759556054)
XLA Ops:
  7.2 0.8 copy-done
  8.1 1.9 %fusion.2 = f32[256,64]{0,1:T(8,128)} fusion(bf16[256,1024]{1,0:T(8,128)(2,1)} %param.5, bf16[1024,64]{0,1:T(8,128)(2,1)S(1)} %copy-done), kind=kOutput, calls=%fused_computation.27 | convolution fusion | flops 33554432 | bytes 720896 | tf_op jit(solution)/shard_map/dot_general | solution.py:41
  11.4 2.4 %scatter_custom_fusion = bf16[384,1024]{1,0:T(8,128)(2,1)S(1)} fusion(s32[256]{0:T(256)S(1)} %compare_select_fusion, bf16[256,1024]{1,0:T(8,128)(2,1)} %param.5, bf16[]{:T(256)} %constant.14.clone.1), kind=kCustom, calls=%fused_computation.1 | custom fusion | bytes 786944 | tf_op jit(solution)/shard_map/scatter | solution.py:16
  14.3 1.2 reduce
  15.6 1.5 reshape.53
  17.0 7.3 %all-to-all-start = ((bf16[8,2,24576]{2,1,0:T(2,128)(2,1)}), bf16[8,2,24576]{2,1,0:T(2,128)(2,1)S(1)}, u32[]{:S(2)}, u32[]{:S(2)}) async-start(bf16[8,2,24576]{2,1,0:T(2,128)(2,1)} %reshape.53), calls=%async_computation | async-start | bytes 1572864 | tf_op jit(solution)/shard_map/all_to_all | solution.py:18
  24.3 20.2 %all-reduce.3.cloned.1.call-done = f32[256,64]{0,1:T(8,128)} async-done(((f32[256,64]{0,1:T(8,128)}), f32[256,64]{0,1:T(8,128)}) %all-reduce.3.cloned.1.call-update) | async-done | bytes 65552 | tf_op jit(solution)/shard_map/psum | solution.py:42
  44.6 0.9 exponential_reduce_fusion
  45.4 1.0 multiply_reduce_fusion.8
  46.4 22.5 %all-reduce = (f32[64]{0:T(128)S(1)}, f32[]{:T(128)}) all-reduce(f32[64]{0:T(128)S(1)} %multiply_reduce_fusion.8, f32[]{:T(128)} %bitcast.1), channel_id=1, replica_groups=mesh['dp'=8,'mp'=4] {'dp'}, use_global_device_ids=true, to_apply=%region_4.0 | all-reduce | flops 65 | bytes 520 | tf_op jit(solution)/shard_map/psum | solution.py:45
  69.6 0.9 multiply_reduce_fusion.7
  70.5 1.0 multiply_reduce_fusion.6
  71.5 17.1 %psum.52 = f32[64]{0:T(128)S(1)} all-reduce(f32[64]{0:T(128)S(1)} %multiply_reduce_fusion.6), channel_id=1, replica_groups=mesh['dp'=8,'mp'=4] {'dp'}, use_global_device_ids=true, to_apply=%region_7.0 | all-reduce | flops 64 | bytes 512 | tf_op jit(solution)/shard_map/psum | solution.py:45
  89.3 0.9 multiply_reduce_fusion.5
  90.2 1.0 multiply_reduce_fusion.4
  91.2 19.1 %psum.53 = f32[64]{0:T(128)S(1)} all-reduce(f32[64]{0:T(128)S(1)} %multiply_reduce_fusion.4), channel_id=1, replica_groups=mesh['dp'=8,'mp'=4] {'dp'}, use_global_device_ids=true, to_apply=%region_10.0 | all-reduce | flops 64 | bytes 512 | tf_op jit(solution)/shard_map/psum | solution.py:45
  111.0 0.9 multiply_reduce_fusion.3
  111.9 1.0 multiply_reduce_fusion.2
  112.9 17.1 %psum.54 = f32[64]{0:T(128)S(1)} all-reduce(f32[64]{0:T(128)S(1)} %multiply_reduce_fusion.2), channel_id=1, replica_groups=mesh['dp'=8,'mp'=4] {'dp'}, use_global_device_ids=true, to_apply=%region_13.0 | all-reduce | flops 64 | bytes 512 | tf_op jit(solution)/shard_map/psum | solution.py:45
  130.7 0.9 multiply_reduce_fusion.1
  131.6 1.0 multiply_reduce_fusion
  132.6 19.1 %psum.55 = f32[64]{0:T(128)S(1)} all-reduce(f32[64]{0:T(128)S(1)} %multiply_reduce_fusion), channel_id=1, replica_groups=mesh['dp'=8,'mp'=4] {'dp'}, use_global_device_ids=true, to_apply=%region_16.0 | all-reduce | flops 64 | bytes 512 | tf_op jit(solution)/shard_map/psum | solution.py:45
  152.4 0.9 select_reduce_fusion
  155.0 1.3 copy.9
  (21 shorter events, 6.2 us)
Async XLA Ops:
  7.2 0.9 copy-start
  7.2 37.4 %all-reduce.3.cloned.1.call-start = ((), (), s32[]{:S(2)}) async-start(), calls=%async_computation.1 | async-start | bytes 131072 | tf_op jit(solution)/shard_map/psum | solution.py:42
  15.6 136.8 %copy-start.1 = (s32[256]{0:T(256)S(1)}, s32[256]{0:T(256)}, u32[]{:S(2)}) copy-start(s32[256]{0:T(256)} %param.8) | copy-start | bytes 3076
  17.0 136.9 %all-to-all-start = ((bf16[8,2,24576]{2,1,0:T(2,128)(2,1)}), bf16[8,2,24576]{2,1,0:T(2,128)(2,1)S(1)}, u32[]{:S(2)}, u32[]{:S(2)}) async-start(bf16[8,2,24576]{2,1,0:T(2,128)(2,1)} %reshape.53), calls=%async_computation | async-start | bytes 1572864 | tf_op jit(solution)/shard_map/all_to_all | solution.py:18
Sparse Core Ops, SparseCore 0:
  10.3 34.2 all-reduce.2
where the time goes:
time: 164 us; the launch traced here: 163 us
  blocking collectives  95 us (58%)
  waiting for transfers between devices  20.3 us (12%)
  other arithmetic  16.1 us (10%)
  between operations  14.8 us (9%)
  local copies, waits for them, and re-layouts  7.63 us (5%)
  starting transfers between devices  7.35 us (4%)
  matrix products  1.95 us (1%)
    psum x5, blocking collectives, group_sum(): return lax.psum(partial_value, 'dp')  95 us
    psum x1, waiting for transfers between devices, local(): logits = lax.psum(partial_logits, 'mp')  20.2 us
    all_to_all x1, starting transfers between devices, dispatch(): lax.all_to_all(buffer[:, None, :], 'dp', split_axis=0, concat_axis=1, til...  7.31 us
    reduce_sum x5, other arithmetic, balance(): jnp.sum(affinity * (weight * row_scale)[:, None], axis=0)  4.8 us
    unnamed x8, local copies, waits for them, and re-layouts  4.71 us
    reduce_sum x5, other arithmetic, balance(): row_scale = experts / jnp.sum(affinity * col_scale[None, :], axis=1)  4.61 us
  transfers between devices with their start and end apart: 2, of which 1 were waited for; matrix products, arithmetic and copies ran while one was open for 13% of the time, Pallas kernels for 0%

commit v1 on v0

v1 whole, which is shorter than its diff:
```python
import functools

import jax
import jax.numpy as jnp
from jax import lax
from jax.experimental import pallas as pl
from jax.experimental.pallas import tpu as pltpu
from jax.sharding import PartitionSpec as P

ITERS = 5
CAP = 6
MESH = pl.DeviceIdType.MESH
F32 = jnp.float32
BF16 = jnp.bfloat16


def iota(shape, dim):
    return lax.broadcasted_iota(jnp.int32, shape, dim)


def kernel(
    n_dp, n_mp, send, early,
    tokens_ref, weight_ref, count_ref, expert_ref, slot_ref,
    gates_ref, out_ref,
    part, part_in, aff, packed, packed_in, meta, meta_in, live,
    p2s, p2r, p3s, p3r, p4s, p4r, bs, br, ms, mr,
):
    rows = tokens_ref.shape[0]
    experts = weight_ref.shape[1]
    share = experts // n_mp
    owned = experts * CAP // n_dp
    lanes = n_dp * send
    i = lax.axis_index("dp")
    j = lax.axis_index("mp")
    few = n_dp <= 16

    def over(low, high, body):
        def step(k, carry):
            body(k)
            return carry
        lax.fori_loop(low, high, step, 0, unroll=few)

    def dp_peer(k):
        return lax.rem(i + k, n_dp)

    def mp_peer(k):
        return lax.rem(j + k, n_mp)

    barrier = pltpu.get_barrier_semaphore()
    over(1, n_dp, lambda k: pl.semaphore_signal(
        barrier, inc=1, device_id={"dp": dp_peer(k)}, device_id_type=MESH))
    for k in range(1, n_mp):
        pl.semaphore_signal(barrier, inc=1, device_id={"mp": mp_peer(k)}, device_id_type=MESH)

    tokens = tokens_ref[...]
    part[...] = lax.dot_general(
        weight_ref[...], tokens, (((0,), (1,)), ((), ())), preferred_element_type=F32)

    count = count_ref[0]
    target = expert_ref[...] * CAP + slot_ref[...]
    first = iota((n_dp, rows), 0) * owned
    offset = target - first
    mine = (offset >= 0) & (offset < owned)
    mine_f = mine.astype(F32)
    before = (iota((rows, rows), 0) < iota((rows, rows), 1)).astype(F32).astype(BF16)
    ranks = jnp.dot(mine_f.astype(BF16), before, preferred_element_type=F32)
    rank = jnp.sum(ranks * mine_f, axis=0, keepdims=True)
    base = jnp.sum(iota((n_dp, rows), 0).astype(F32) * mine_f, axis=0, keepdims=True)
    is_live = iota((1, rows), 1) < count
    value = jnp.where(mine & is_live, offset + 1, 0).astype(F32)
    column = (rank + (i * send).astype(F32)).astype(jnp.int32)
    spread = (iota((lanes, rows), 0) == column).astype(F32).astype(BF16)
    table = lax.dot_general(
        value.astype(BF16), spread, (((1,), (1,)), ((), ())), preferred_element_type=F32)
    for o in range(n_dp):
        meta[o, :, :lanes] = table[o:o + 1, :]
        meta[o, :, lanes:] = jnp.full((1, 128), count.astype(F32), F32)
    place = jnp.where(is_live, (base * send + rank).astype(jnp.int32), -1)
    chunk = min(lanes, 256)
    for top in range(0, lanes, chunk):
        pick = (iota((chunk, rows), 0) + top == place).astype(F32).astype(BF16)
        packed[top:top + chunk, :] = jnp.dot(
            pick, tokens, preferred_element_type=F32).astype(BF16)

    pl.semaphore_wait(barrier, n_dp + n_mp - 2)

    def span(index, size):
        return pl.ds(pl.multiple_of(index * size, size), size)

    def p2(peer, at):
        return pltpu.make_async_remote_copy(
            src_ref=part.at[span(peer, share)], dst_ref=part_in.at[at],
            send_sem=p2s.at[peer], recv_sem=p2r.at[at],
            device_id={"mp": peer}, device_id_type=MESH)

    def p3(peer, at):
        block = aff.at[at, span(j, share)]
        return pltpu.make_async_remote_copy(
            src_ref=block, dst_ref=block, send_sem=p3s.at[peer], recv_sem=p3r.at[at],
            device_id={"dp": peer}, device_id_type=MESH)

    def p4(peer, at, group):
        block = aff.at[group, span(at, share)]
        return pltpu.make_async_remote_copy(
            src_ref=block, dst_ref=block,
            send_sem=p4s.at[peer, group], recv_sem=p4r.at[at, group],
            device_id={"mp": peer}, device_id_type=MESH)

    def bulk(peer, at):
        return pltpu.make_async_remote_copy(
            src_ref=packed.at[span(peer, send)], dst_ref=packed_in.at[span(at, send)],
            send_sem=bs.at[peer], recv_sem=br.at[at],
            device_id={"dp": peer}, device_id_type=MESH)

    def note(peer, at):
        return pltpu.make_async_remote_copy(
            src_ref=meta.at[peer], dst_ref=meta_in.at[at],
            send_sem=ms.at[peer], recv_sem=mr.at[at],
            device_id={"dp": peer}, device_id_type=MESH)

    for k in range(1, n_mp):
        p2(mp_peer(k), j).start()
    over(1, n_dp, lambda k: note(dp_peer(k), i).start())
    split = min(early + 1, n_dp)
    over(1, split, lambda k: bulk(dp_peer(k), i).start())

    total_logits = part[span(j, share), :]
    for k in range(1, n_mp):
        src = mp_peer(k)
        p2(src, src).wait_recv()
        total_logits = total_logits + part_in[src]
    aff[i, span(j, share), :] = jnp.exp(total_logits)
    over(1, n_dp, lambda k: p3(dp_peer(k), i).start())
    for k in range(1, n_mp):
        p4(mp_peer(k), j, i).start()
    over(split, n_dp, lambda k: bulk(dp_peer(k), i).start())

    packed_in[span(i, send), :] = packed[span(i, send), :]
    meta_in[i] = meta[i]

    def forward(k):
        src = lax.rem(i + n_dp - k, n_dp)
        p3(src, src).wait_recv()
        for m in range(1, n_mp):
            p4(mp_peer(m), j, src).start()
    over(1, n_dp, forward)

    over(1, n_dp, lambda k: note(dp_peer(k), dp_peer(k)).wait_recv())
    where_to = jnp.zeros((1, lanes), F32)
    total = jnp.zeros((1, 1), F32)
    for g in range(n_dp):
        value = meta_in[g, :, :lanes]
        where_to = where_to + jnp.where(value > 0, (value - 1) * n_dp + (g + 1), 0.0)
        held = meta_in[g, :, lanes:lanes + 1]
        total = total + held
        live[g] = (iota((1, rows), 1).astype(F32) < held).astype(F32)
    place_in = (where_to - 1).astype(jnp.int32)
    unpack = (iota((owned * n_dp, lanes), 0) == place_in).astype(F32).astype(BF16)

    def landed(k):
        for m in range(1, n_mp):
            src = mp_peer(m)
            p4(src, src, dp_peer(k)).wait_recv()
    over(0, n_dp, landed)

    col_scale = jnp.ones((experts, 1), F32)
    last = col_scale
    for sweep in range(ITERS):
        last = col_scale
        scale = jnp.broadcast_to(last, (experts, rows))

        def add_group(g, acc, scale=scale):
            block = aff[g]
            row_scale = experts / jnp.sum(block * scale, axis=0, keepdims=True)
            return acc + block * (live[g] * row_scale)
        acc = lax.fori_loop(0, n_dp, add_group, jnp.zeros((experts, rows), F32), unroll=few)
        col_scale = total / jnp.sum(acc, axis=1, keepdims=True)

    block = aff[i]
    row_scale = experts / jnp.sum(block * last, axis=0, keepdims=True)
    chosen = expert_ref[...] == iota((experts, rows), 0)
    picked = jnp.sum(jnp.where(chosen, block * col_scale, 0.0), axis=0, keepdims=True)
    gates_ref[...] = live[i] * row_scale * picked

    over(1, n_dp, lambda k: bulk(dp_peer(k), dp_peer(k)).wait_recv())
    out_ref[...] = jnp.dot(unpack, packed_in[...], preferred_element_type=F32).astype(BF16)

    for k in range(1, n_mp):
        p2(mp_peer(k), j).wait_send()

    def drained(k):
        p3(dp_peer(k), i).wait_send()
        bulk(dp_peer(k), i).wait_send()
        note(dp_peer(k), i).wait_send()
    over(1, n_dp, drained)

    def forwarded(k):
        for m in range(1, n_mp):
            p4(mp_peer(m), j, dp_peer(k)).wait_send()
    over(0, n_dp, forwarded)


EARLY = 0


def solution(mesh):
    n_dp, n_mp = mesh.shape["dp"], mesh.shape["mp"]

    def local(tokens, router_weight, valid_count, expert_id, slot_id):
        rows, width = tokens.shape
        experts = router_weight.shape[1]
        share = experts // n_mp
        send = -(-(rows // n_dp) // 16) * 16
        lanes = n_dp * send
        slots = experts * CAP // n_dp
        vmem = pl.BlockSpec(memory_space=pltpu.VMEM)
        dma = pltpu.SemaphoreType.DMA
        gates, out = pl.pallas_call(
            functools.partial(kernel, n_dp, n_mp, send, EARLY),
            out_shape=(
                jax.ShapeDtypeStruct((1, rows), F32),
                jax.ShapeDtypeStruct((slots * n_dp, width), BF16),
            ),
            in_specs=[vmem, vmem, pl.BlockSpec(memory_space=pltpu.SMEM), vmem, vmem],
            out_specs=(vmem, vmem),
            scratch_shapes=[
                pltpu.VMEM((experts, rows), F32),
                pltpu.VMEM((n_mp, share, rows), F32),
                pltpu.VMEM((n_dp, experts, rows), F32),
                pltpu.VMEM((lanes, width), BF16),
                pltpu.VMEM((lanes, width), BF16),
                pltpu.VMEM((n_dp, 1, lanes + 128), F32),
                pltpu.VMEM((n_dp, 1, lanes + 128), F32),
                pltpu.VMEM((n_dp, 1, rows), F32),
                dma((n_mp,)), dma((n_mp,)), dma((n_dp,)), dma((n_dp,)),
                dma((n_mp, n_dp)), dma((n_mp, n_dp)),
                dma((n_dp,)), dma((n_dp,)), dma((n_dp,)), dma((n_dp,)),
            ],
            compiler_params=pltpu.CompilerParams(
                collective_id=0, has_side_effects=True, vmem_limit_bytes=60 * 1024 * 1024),
        )(tokens, router_weight, valid_count, expert_id.reshape(1, rows), slot_id.reshape(1, rows))
        return gates.reshape(rows), out.reshape(slots, n_dp, width)

    placed = (P("dp", "mp"), P("mp", None), P("dp"), P("dp"), P("dp"))
    return jax.shard_map(
        local, mesh=mesh, in_specs=placed, out_specs=(P("dp"), P("dp", None, "mp")), check_vma=False
    )
```

time: 164 us -> 32.8 us (0.20)
  the two profiles are of different devices: /device:TPU:0 before, /device:TPU:13 now
where the time goes in v1:
time: 32.8 us; the launch traced here: 32.6 us
  Pallas kernels  26.3 us (80%)
  local copies, waits for them, and re-layouts  5.02 us (15%)
  between operations  1.29 us (4%)
    pallas_call x1, Pallas kernels, local(): pl.pallas_call(functools.partial(kernel, n_dp, n_mp, send, EARLY), out_sh...  26.3 us
    unnamed x5, local copies, waits for them, and re-layouts  5.02 us

profile of v1, /device:TPU:13, one launch (start us, length us, event | category | flops | bytes accessed | tf_op | source)
XLA Modules:
  0.0 32.6 jit_solution(3539416670823830250)
XLA Ops:
  1.3 1.7 %copy.7.weight_ref = bf16[1024,64]{1,0:T(8,128)(2,1)} copy(bf16[1024,64]{0,1:T(8,128)(2,1)} %param.6) | data formatting | bytes 262144 | tf_op args[1]
  3.0 26.3 %shard_map.68 = (f32[1,256]{1,0:T(1,128)}, bf16[384,1024]{1,0:T(8,128)(2,1)}) custom-call(bf16[256,1024]{1,0:T(8,128)(2,1)} %tokens_ref.1, bf16[1024,64]{1,0:T(8,128)(2,1)} %copy.7.weight_ref, s32[1]{0:T(128)S(6)} %copy.10.count_ref, s32[1,256]{1,0:T(1,128)} %bitcast.5, s32[1,256]{1,0:T(1,128)} %bitcast.6), custom_call_target="tpu_custom_call" | custom-call | tf_op jit(solution)/shard_map/pallas_call | solution.py:218
  29.3 0.0 copy-start
  29.3 0.6 %copy-done = f32[1,256]{1,0:T(1,128)S(1)} copy-done((f32[1,256]{1,0:T(1,128)S(1)}, f32[1,256]{1,0:T(1,128)}, u32[]{:S(2)}) %copy-start) | copy-done | bytes 1048
  29.9 0.6 %copy.11 = f32[256]{0:T(256)} copy(f32[256]{0:T(256)S(1)} %bitcast.7) | data formatting | bytes 2048
  30.5 2.1 %copy.12 = bf16[48,8,1024]{2,1,0:T(8,128)(2,1)} copy(bf16[48,8,1024]{2,1,0:T(8,128)(2,1)} %bitcast.4) | data formatting | bytes 1572864
Async XLA Ops:
  29.3 0.7 %copy-start = (f32[1,256]{1,0:T(1,128)S(1)}, f32[1,256]{1,0:T(1,128)}, u32[]{:S(2)}) copy-start(f32[1,256]{1,0:T(1,128)} %get-tuple-element.4) | copy-start | bytes 3076

commit v2 on v1

--- a/solution.py
+++ b/solution.py
@@ -20,13 +20,13 @@
 
 def kernel(
     n_dp, n_mp, send, early,
-    tokens_ref, weight_ref, count_ref, expert_ref, slot_ref,
-    gates_ref, out_ref,
-    part, part_in, aff, packed, packed_in, meta, meta_in, live,
-    p2s, p2r, p3s, p3r, p4s, p4r, bs, br, ms, mr,
+    tokens_hbm, weight_hbm, count_ref, expert_hbm, slot_hbm,
+    gates_ref, place_ref, packed_in,
+    tokens_ref, weight_ref, expert_ref, slot_ref, part, part_in, aff, packed, meta, meta_in, live,
+    own, p2s, p2r, p3s, p3r, p4s, p4r, bs, br, ms, mr,
 ):
     rows = tokens_ref.shape[0]
-    experts = weight_ref.shape[1]
+    experts = weight_ref.shape[0]
     share = experts // n_mp
     owned = experts * CAP // n_dp
     lanes = n_dp * send
@@ -46,16 +46,23 @@
     def mp_peer(k):
         return lax.rem(j + k, n_mp)
 
+    fetches = [
+        pltpu.make_async_copy(src, dst, own.at[n])
+        for n, (src, dst) in enumerate((
+            (tokens_hbm, tokens_ref), (weight_hbm, weight_ref),
+            (expert_hbm, expert_ref), (slot_hbm, slot_ref)))
+    ]
+    for fetch in fetches:
+        fetch.start()
+
     barrier = pltpu.get_barrier_semaphore()
     over(1, n_dp, lambda k: pl.semaphore_signal(
         barrier, inc=1, device_id={"dp": dp_peer(k)}, device_id_type=MESH))
     for k in range(1, n_mp):
         pl.semaphore_signal(barrier, inc=1, device_id={"mp": mp_peer(k)}, device_id_type=MESH)
 
-    tokens = tokens_ref[...]
-    part[...] = lax.dot_general(
-        weight_ref[...], tokens, (((0,), (1,)), ((), ())), preferred_element_type=F32)
-
+    fetches[2].wait()
+    fetches[3].wait()
     count = count_ref[0]
     target = expert_ref[...] * CAP + slot_ref[...]
     first = iota((n_dp, rows), 0) * owned
@@ -76,6 +83,13 @@
         meta[o, :, :lanes] = table[o:o + 1, :]
         meta[o, :, lanes:] = jnp.full((1, 128), count.astype(F32), F32)
     place = jnp.where(is_live, (base * send + rank).astype(jnp.int32), -1)
+
+    fetches[0].wait()
+    fetches[1].wait()
+    tokens = tokens_ref[...]
+    part[...] = lax.dot_general(
+        weight_ref[...], tokens, (((1,), (1,)), ((), ())), preferred_element_type=F32)
+
     chunk = min(lanes, 256)
     for top in range(0, lanes, chunk):
         pick = (iota((chunk, rows), 0) + top == place).astype(F32).astype(BF16)
@@ -99,11 +113,17 @@
             src_ref=block, dst_ref=block, send_sem=p3s.at[peer], recv_sem=p3r.at[at],
             device_id={"dp": peer}, device_id_type=MESH)
 
-    def p4(peer, at, group):
+    pair = j + 1 - 2 * lax.rem(j, 2)
+
+    def direct():
+        return [lax.rem(j + 2 * m, n_mp) for m in range(1, n_mp // 2)]
+
+    def p4(peer, at, group, lane=None):
         block = aff.at[group, span(at, share)]
+        lane = peer if lane is None else lane
         return pltpu.make_async_remote_copy(
             src_ref=block, dst_ref=block,
-            send_sem=p4s.at[peer, group], recv_sem=p4r.at[at, group],
+            send_sem=p4s.at[lane, group], recv_sem=p4r.at[at, group],
             device_id={"mp": peer}, device_id_type=MESH)
 
     def bulk(peer, at):
@@ -120,6 +140,7 @@
 
     for k in range(1, n_mp):
         p2(mp_peer(k), j).start()
+
     over(1, n_dp, lambda k: note(dp_peer(k), i).start())
     split = min(early + 1, n_dp)
     over(1, split, lambda k: bulk(dp_peer(k), i).start())
@@ -131,19 +152,31 @@
         total_logits = total_logits + part_in[src]
     aff[i, span(j, share), :] = jnp.exp(total_logits)
     over(1, n_dp, lambda k: p3(dp_peer(k), i).start())
-    for k in range(1, n_mp):
-        p4(mp_peer(k), j, i).start()
+    for peer in direct() + [pair]:
+        p4(peer, j, i).start()
     over(split, n_dp, lambda k: bulk(dp_peer(k), i).start())
 
-    packed_in[span(i, send), :] = packed[span(i, send), :]
+    keep = pltpu.make_async_copy(
+        packed.at[span(i, send)], packed_in.at[span(i, send)], own.at[4])
+    keep.start()
     meta_in[i] = meta[i]
 
     def forward(k):
         src = lax.rem(i + n_dp - k, n_dp)
         p3(src, src).wait_recv()
-        for m in range(1, n_mp):
-            p4(mp_peer(m), j, src).start()
+        for peer in direct() + [pair]:
+            p4(peer, j, src).start()
     over(1, n_dp, forward)
+
+    def across(peer):
+        return peer + 1 - 2 * lax.rem(peer, 2)
+
+    def relay(k):
+        group = lax.rem(i + n_dp - k, n_dp)
+        for src in direct():
+            p4(src, src, group).wait_recv()
+            p4(pair, src, group, across(src)).start()
+    over(0, n_dp, relay)
 
     over(1, n_dp, lambda k: note(dp_peer(k), dp_peer(k)).wait_recv())
     where_to = jnp.zeros((1, lanes), F32)
@@ -154,13 +187,11 @@
         held = meta_in[g, :, lanes:lanes + 1]
         total = total + held
         live[g] = (iota((1, rows), 1).astype(F32) < held).astype(F32)
-    place_in = (where_to - 1).astype(jnp.int32)
-    unpack = (iota((owned * n_dp, lanes), 0) == place_in).astype(F32).astype(BF16)
+    place_ref[...] = (where_to - 1).astype(jnp.int32)
 
     def landed(k):
-        for m in range(1, n_mp):
-            src = mp_peer(m)
-            p4(src, src, dp_peer(k)).wait_recv()
+        for src in [pair] + [across(peer) for peer in direct()]:
+            p4(pair, src, dp_peer(k)).wait_recv()
     over(0, n_dp, landed)
 
     col_scale = jnp.ones((experts, 1), F32)
@@ -183,7 +214,7 @@
     gates_ref[...] = live[i] * row_scale * picked
 
     over(1, n_dp, lambda k: bulk(dp_peer(k), dp_peer(k)).wait_recv())
-    out_ref[...] = jnp.dot(unpack, packed_in[...], preferred_element_type=F32).astype(BF16)
+    keep.wait()
 
     for k in range(1, n_mp):
         p2(mp_peer(k), j).wait_send()
@@ -195,12 +226,25 @@
     over(1, n_dp, drained)
 
     def forwarded(k):
-        for m in range(1, n_mp):
-            p4(mp_peer(m), j, dp_peer(k)).wait_send()
+        for peer in direct() + [pair]:
+            p4(peer, j, dp_peer(k)).wait_send()
+        for src in direct():
+            p4(pair, src, dp_peer(k), across(src)).wait_send()
     over(0, n_dp, forwarded)
 
 
-EARLY = 0
+def unpack(chunk, gates_in, place_ref, packed_ref, gates_ref, out_ref):
+    gates_ref[...] = gates_in[...]
+    at = iota((chunk, packed_ref.shape[0]), 0) + pl.program_id(0) * chunk
+    pick = (at == place_ref[...]).astype(F32).astype(BF16)
+    out_ref[...] = jnp.dot(pick, packed_ref[...], preferred_element_type=F32).astype(BF16)
+
+
+EARLY = 2
+CHUNK = 192
+VMEM = 67043328
+ROOM = 64
+SMALL = 16 * 1024 * 1024
 
 
 def solution(mesh):
@@ -213,32 +257,55 @@
         send = -(-(rows // n_dp) // 16) * 16
         lanes = n_dp * send
         slots = experts * CAP // n_dp
+        total = slots * n_dp
+        chunk = max(c for c in range(16, CHUNK + 1, 16) if total % c == 0)
+        limit = VMEM - lanes * width * 2 - ROOM * 1024
+        hbm = pl.BlockSpec(memory_space=pltpu.HBM)
+        anywhere = pl.BlockSpec(memory_space=pl.ANY)
         vmem = pl.BlockSpec(memory_space=pltpu.VMEM)
         dma = pltpu.SemaphoreType.DMA
-        gates, out = pl.pallas_call(
+        gates, place, packed = pl.pallas_call(
             functools.partial(kernel, n_dp, n_mp, send, EARLY),
             out_shape=(
-                jax.ShapeDtypeStruct((1, rows), F32),
-                jax.ShapeDtypeStruct((slots * n_dp, width), BF16),
+                pltpu.VMEM((1, rows), F32),
+                pltpu.VMEM((1, lanes), jnp.int32),
+                pltpu.VMEM((lanes, width), BF16),
             ),
-            in_specs=[vmem, vmem, pl.BlockSpec(memory_space=pltpu.SMEM), vmem, vmem],
-            out_specs=(vmem, vmem),
+            in_specs=[hbm, hbm, pl.BlockSpec(memory_space=pltpu.SMEM), hbm, hbm],
+            out_specs=(vmem, vmem, anywhere),
             scratch_shapes=[
+                pltpu.VMEM((rows, width), BF16),
+                pltpu.VMEM((experts, width), BF16),
+                pltpu.VMEM((1, rows), jnp.int32),
+                pltpu.VMEM((1, rows), jnp.int32),
                 pltpu.VMEM((experts, rows), F32),
                 pltpu.VMEM((n_mp, share, rows), F32),
                 pltpu.VMEM((n_dp, experts, rows), F32),
                 pltpu.VMEM((lanes, width), BF16),
-                pltpu.VMEM((lanes, width), BF16),
                 pltpu.VMEM((n_dp, 1, lanes + 128), F32),
                 pltpu.VMEM((n_dp, 1, lanes + 128), F32),
                 pltpu.VMEM((n_dp, 1, rows), F32),
-                dma((n_mp,)), dma((n_mp,)), dma((n_dp,)), dma((n_dp,)),
+                dma((5,)), dma((n_mp,)), dma((n_mp,)), dma((n_dp,)), dma((n_dp,)),
                 dma((n_mp, n_dp)), dma((n_mp, n_dp)),
                 dma((n_dp,)), dma((n_dp,)), dma((n_dp,)), dma((n_dp,)),
             ],
             compiler_params=pltpu.CompilerParams(
-                collective_id=0, has_side_effects=True, vmem_limit_bytes=60 * 1024 * 1024),
-        )(tokens, router_weight, valid_count, expert_id.reshape(1, rows), slot_id.reshape(1, rows))
+                collective_id=0, has_side_effects=True, vmem_limit_bytes=limit),
+        )(tokens, router_weight.T, valid_count, expert_id.reshape(1, rows), slot_id.reshape(1, rows))
+        whole = lambda b: (0, 0)
+        gates, out = pl.pallas_call(
+            functools.partial(unpack, chunk),
+            grid=(total // chunk,),
+            out_shape=(
+                jax.ShapeDtypeStruct((1, rows), F32),
+                jax.ShapeDtypeStruct((total, width), BF16),
+            ),
+            in_specs=[
+                pl.BlockSpec((1, rows), whole), pl.BlockSpec((1, lanes), whole), vmem],
+            out_specs=(
+                pl.BlockSpec((1, rows), whole), pl.BlockSpec((chunk, width), lambda b: (b, 0))),
+            compiler_params=pltpu.CompilerParams(vmem_limit_bytes=SMALL),
+        )(gates, place, packed)
         return gates.reshape(rows), out.reshape(slots, n_dp, width)
 
     placed = (P("dp", "mp"), P("mp", None), P("dp"), P("dp"), P("dp"))

time: 32.8 us -> 25.4 us (0.77)
  local copies, waits for them, and re-layouts: 5.02 us -> 0 us
  Pallas kernels: 26.3 us -> 23.7 us
    unnamed x5 -> x0, local copies, waits for them, and re-layouts: 5.02 us -> none
    pallas_call x1, Pallas kernels: 26.3 us -> 22.3 us  [local(): pl.pallas_call(functools.partial(kernel, n_dp, n_mp, send, EARLY), out_sh...]
    pallas_call x0 -> x1, Pallas kernels: none -> 1.32 us  [local(): pl.pallas_call(functools.partial(unpack, chunk), grid=(total // chunk,),...]
where the time goes in v2:
time: 25.4 us; the launch traced here: 24.9 us
  Pallas kernels  23.7 us (93%)
  between operations  1.28 us (5%)
    pallas_call x1, Pallas kernels, local(): pl.pallas_call(functools.partial(kernel, n_dp, n_mp, send, EARLY), out_sh...  22.3 us
    pallas_call x1, Pallas kernels, local(): pl.pallas_call(functools.partial(unpack, chunk), grid=(total // chunk,),...  1.32 us

profile of v2, /device:TPU:13, one launch (start us, length us, event | category | flops | bytes accessed | tf_op | source)
XLA Modules:
  0.0 24.9 jit_solution(12993832461650820695)
XLA Ops:
  1.3 22.3 %shard_map.68 = (f32[1,256]{1,0:T(1,128)S(1)}, s32[1,256]{1,0:T(1,128)S(1)}, bf16[256,1024]{1,0:T(8,128)(2,1)S(1)}) custom-call(bf16[256,1024]{1,0:T(8,128)(2,1)} %tokens_hbm.1, bf16[64,1024]{1,0:T(8,128)(2,1)} %bitcast.5, s32[1]{0:T(128)S(6)} %copy.7.count_ref, s32[1,256]{1,0:T(1,128)} %bitcast.6, s32[1,256]{1,0:T(1,128)} %bitcast.7), custom_call_target="tpu_custom_call" | custom-call | tf_op jit(solution)/shard_map/pallas_call | solution.py:267
  23.6 1.3 %shard_map.69 = (f32[1,256]{1,0:T(1,128)}, bf16[384,1024]{1,0:T(8,128)(2,1)}) custom-call(f32[1,256]{1,0:T(1,128)S(1)} %get-tuple-element.7.gates_in, s32[1,256]{1,0:T(1,128)S(1)} %get-tuple-element.8.place_ref, bf16[256,1024]{1,0:T(8,128)(2,1)S(1)} %get-tuple-element.9.packed_ref), custom_call_target="tpu_custom_call" | custom-call | tf_op jit(solution)/shard_map/pallas_call | solution.py:296

commit v3 on v2

--- a/solution.py
+++ b/solution.py
@@ -141,9 +141,9 @@
     for k in range(1, n_mp):
         p2(mp_peer(k), j).start()
 
-    over(1, n_dp, lambda k: note(dp_peer(k), i).start())
     split = min(early + 1, n_dp)
     over(1, split, lambda k: bulk(dp_peer(k), i).start())
+    over(1, n_dp, lambda k: note(dp_peer(k), i).start())
 
     total_logits = part[span(j, share), :]
     for k in range(1, n_mp):

time: 25.4 us -> 25.4 us (level)
  no operation moved by 1% of the time
where the time goes in v3:
time: 25.4 us; the launch traced here: 24.9 us
  Pallas kernels  23.7 us (93%)
  between operations  1.28 us (5%)
    pallas_call x1, Pallas kernels, local(): pl.pallas_call(functools.partial(kernel, n_dp, n_mp, send, EARLY), out_sh...  22.3 us
    pallas_call x1, Pallas kernels, local(): pl.pallas_call(functools.partial(unpack, chunk), grid=(total // chunk,),...  1.32 us

profile of v3, /device:TPU:13, one launch (start us, length us, event | category | flops | bytes accessed | tf_op | source)
XLA Modules:
  0.0 24.9 jit_solution(7523317635169724367)
XLA Ops:
  1.3 22.3 %shard_map.68 = (f32[1,256]{1,0:T(1,128)S(1)}, s32[1,256]{1,0:T(1,128)S(1)}, bf16[256,1024]{1,0:T(8,128)(2,1)S(1)}) custom-call(bf16[256,1024]{1,0:T(8,128)(2,1)} %tokens_hbm.1, bf16[64,1024]{1,0:T(8,128)(2,1)} %bitcast.5, s32[1]{0:T(128)S(6)} %copy.7.count_ref, s32[1,256]{1,0:T(1,128)} %bitcast.6, s32[1,256]{1,0:T(1,128)} %bitcast.7), custom_call_target="tpu_custom_call" | custom-call | tf_op jit(solution)/shard_map/pallas_call | solution.py:267
  23.6 1.3 %shard_map.69 = (f32[1,256]{1,0:T(1,128)}, bf16[384,1024]{1,0:T(8,128)(2,1)}) custom-call(f32[1,256]{1,0:T(1,128)S(1)} %get-tuple-element.7.gates_in, s32[1,256]{1,0:T(1,128)S(1)} %get-tuple-element.8.place_ref, bf16[256,1024]{1,0:T(8,128)(2,1)S(1)} %get-tuple-element.9.packed_ref), custom_call_target="tpu_custom_call" | custom-call | tf_op jit(solution)/shard_map/pallas_call | solution.py:296
